TPU v7x, 256 devices: a whole 4x4x8 slice. The times are simulated.
256 devices in a mesh: seq: 64 (over x, z, core), head: 4 (over y).
Axes of the slice: x: 4, y: 4, z: 8, core: 2. Of those that a mesh axis runs over, the one named last changes fastest.
Arguments:
- inputs: float32 [32768, 5120], P('seq', 'head'), may hold values from -3 to 3
- log_decay: float32 [80, 32768], P('head', 'seq'), may hold values from -1 to 0, as said below
- b_proj: float32 [32768, 128], P('seq'), may hold values from -0.5 to 0.5
- c_proj: float32 [32768, 128], P('seq'), may hold values from -0.5 to 0.5
- entry_states: float32 [64, 80, 64, 128], P('seq', 'head'), may hold values from -12 to 12
- out_grad: float32 [32768, 5120], P('seq', 'head'), may hold values from -3 to 3
Outputs:
- d_inputs: float32 [32768, 5120], P('seq', 'head')
- d_log_decay: float32 [80, 32768], P('head', 'seq')
- d_b_proj: float32 [32768, 128], P('seq')
- d_c_proj: float32 [32768, 128], P('seq')
- entry_grad: float32 [64, 80, 64, 128], P('seq', 'head')
Inputs may be any that keep to these rules, and one draw needn't show every extreme that they name: `log_decay`: negative everywhere.
All inputs are finite; a program needn't handle non-finite values.
Results may differ from a plain program's by a relative error of at most 0.0003.
Values sent between devices are 32-bit elements; how exact they have to be, the bound alone decides.
A program may use at most 192 MiB of HBM per device.

v0:
```python
import functools

import jax
import jax.numpy as jnp
from jax import lax
from jax.experimental import pallas as pl
from jax.experimental.pallas import tpu as pltpu
from jax.sharding import PartitionSpec as P

F32 = jnp.float32
BF16 = jnp.bfloat16
MESH = pl.DeviceIdType.MESH
TOK = 512
HEADS = 20
WIDTH = 64
STATE = 128
ROWS = HEADS * WIDTH
PAIRS = HEADS // 2
TILE = 128
LOG2E = 1.4426950408889634
ZN = 8
XN = 4
HN = 4
HALF = STATE // 2
SLICE = HALF // ZN


def split(v):
    hi = v.astype(BF16)
    return hi, (v - hi.astype(F32)).astype(BF16)


def split3(v):
    hi = v.astype(BF16)
    rest = v - hi.astype(F32)
    mid = rest.astype(BF16)
    return hi, mid, (rest - mid.astype(F32)).astype(BF16)


def nn(a, b):
    return lax.dot_general(a, b, (((1,), (0,)), ((), ())), preferred_element_type=F32)


def nt(a, b):
    return lax.dot_general(a, b, (((1,), (1,)), ((), ())), preferred_element_type=F32)


def nn3(a, b):
    a_hi, a_lo = a
    b_hi, b_lo = b
    width = b_hi.shape[1]
    both = nn(a_hi, jnp.concatenate([b_hi, b_lo], axis=1))
    return both[:, :width] + both[:, width:] + nn(a_lo, b_hi)


def nt3(a, b):
    a_hi, a_lo = a
    b_hi, b_lo = b
    return nt(a_hi, b_hi) + nt(a_hi, b_lo) + nt(a_lo, b_hi)


def iota(shape, dim):
    return lax.broadcasted_iota(jnp.int32, shape, dim)


def prefix_sums(value, strict):
    rows = value.shape[0]
    a, b = iota((TILE, TILE), 0), iota((TILE, TILE), 1)
    upper = jnp.where(a < b if strict else a <= b, 1.0, 0.0).astype(BF16)
    tiles = []
    base = jnp.zeros((rows, 1), F32)
    for j in range(TOK // TILE):
        part = value[:, j * TILE : (j + 1) * TILE]
        hi, mid, lo = split3(part)
        inner = nn(hi, upper) + nn(mid, upper) + nn(lo, upper)
        tiles.append(inner + base)
        last = tiles[-1][:, TILE - 1 : TILE]
        base = last + part[:, TILE - 1 : TILE] if strict else last
    return jnp.concatenate(tiles, axis=1)


def pair_picker():
    row, lane = iota((8, TILE), 0), iota((8, TILE), 1)
    low = (row == 0) & (lane < WIDTH)
    high = (row == 1) & (lane >= WIDTH)
    return jnp.where(low | high, 1.0, 0.0).astype(BF16)


def local_kernel(
    x_ref, ld_ref, b_ref, c_ref, s0_ref, dy_ref,
    gt_ref, a_ref, l3_ref, dx_ref, txh_ref, txl_ref, tail_ref, v_ref, db_ref, dc_ref,
    ld32, lx, lrow, cbt, et, eh, el,
):
    first = iota((1, TILE), 1) < WIDTH
    ld32[...] = jnp.zeros_like(ld32)
    ld32[0:HEADS, :] = ld_ref[...] * LOG2E
    cum = prefix_sums(ld32[...], False)
    for h in range(HEADS):
        lrow[h] = cum[h : h + 1, :]
    hi, mid, lo = split3(cum)
    stack = jnp.concatenate(
        [hi.astype(F32), mid.astype(F32), lo.astype(F32), jnp.zeros_like(cum)], axis=0
    )
    columns = stack.T
    l3_ref[...] = columns[TOK - 1 : TOK, :]
    columns = columns.astype(BF16)
    spread = jnp.where(
        (iota((TILE, HEADS * TILE), 0) & 31) == (iota((TILE, HEADS * TILE), 1) >> 7), 1.0, 0.0
    ).astype(BF16)
    for k in range(HEADS // 4):
        part = slice(k * 4 * TILE, (k + 1) * 4 * TILE)
        lx[:, part] = nn(columns, spread[:, part])

    c_pair = split(c_ref[...])
    ct_pair = split(c_ref[...].T)
    b_pair = split(b_ref[...])

    def start(p, carry):
        tile = pl.ds(pl.multiple_of(p * TILE, TILE), TILE)
        la = lx[:, pl.ds(pl.multiple_of(p * 2 * TILE, TILE), TILE)]
        lb = lx[:, pl.ds(pl.multiple_of(p * 2 * TILE + TILE, TILE), TILE)]
        both = jnp.where(first, la, lb)
        e_pair = split(jnp.exp2(both) * dy_ref[:, tile])
        eh[:, tile] = e_pair[0]
        el[:, tile] = e_pair[1]
        gt_ref[:, tile] = nn3(ct_pair, e_pair)
        end = both[TOK - 1 : TOK, :]
        a_ref[:, tile] = jnp.exp2(end)
        tail = jnp.exp2(end - both)
        tail_ref[:, tile] = tail
        tx = split(tail * x_ref[:, tile])
        txh_ref[:, tile] = tx[0]
        txl_ref[:, tile] = tx[1]
        return carry

    lax.fori_loop(0, PAIRS, start, 0)

    causal = iota((TOK, TOK), 0) <= iota((TOK, TOK), 1)
    cbt[...] = jnp.where(causal, nt3(b_pair, c_pair), 0.0)
    et[...] = jnp.zeros_like(et)
    picker = pair_picker()
    sub = iota((8, TOK), 0)

    def inner(p, carry):
        tile = pl.ds(pl.multiple_of(p * TILE, TILE), TILE)
        x, dy = x_ref[:, tile], dy_ref[:, tile]
        xh, xl = split(x)
        dyh, dyl = split(dy)
        xh_f, dyh_f = xh.astype(F32), dyh.astype(F32)
        x_turn = pltpu.roll(xl.astype(F32), WIDTH, 1)
        dy_turn = pltpu.roll(dyh_f, WIDTH, 1)
        dyl_f = dyl.astype(F32)
        zero = jnp.zeros_like(x)
        dycat = jnp.concatenate([dyh, dyl], axis=1)
        left, right, turn = [], [], []
        for k in range(2):
            here = first if k == 0 else jnp.logical_not(first)
            left.append(
                jnp.concatenate(
                    [jnp.where(here, xh_f, x_turn), jnp.where(here, xh_f, zero)], axis=1
                ).astype(BF16)
            )
            right.append(
                jnp.concatenate(
                    [jnp.where(here, dyh_f, dy_turn), jnp.where(here, dyl_f, zero)], axis=1
                ).astype(BF16)
            )
        z = [[jnp.zeros((1, TILE), F32) for j in range(4)] for k in range(2)]
        for i in range(4):
            r = i * TILE
            mix = cbt[r : r + TILE, r:]
            outs = []
            gained = et[r : r + TILE, r:]
            for k in range(2):
                grad = nt(left[k][r : r + TILE], right[k][r:])
                column = lx[r : r + TILE, pl.ds(pl.multiple_of((2 * p + k) * TILE, TILE), TILE)]
                row = lrow[2 * p + k][:, r:]
                decay = []
                for j in range(4 - i):
                    gap = row[:, j * TILE : (j + 1) * TILE] - column
                    decay.append(jnp.exp2(jnp.minimum(gap, 0.0) if j == 0 else gap))
                decay = jnp.concatenate(decay, axis=1)
                weight = decay * mix
                gained = gained + decay * grad
                sums = jnp.sum(weight * grad, axis=0, keepdims=True)
                for j in range(4 - i):
                    z[k][i + j] = z[k][i + j] + sums[:, j * TILE : (j + 1) * TILE]
                wh, wl = split(weight)
                wide = nn(wh, dycat[r:])
                outs.append(wide[:, :TILE] + wide[:, TILE:] + nn(wl, dyh[r:]))
            et[r : r + TILE, r:] = gained
            dx_ref[r : r + TILE, tile] = jnp.where(first, outs[0], outs[1])
        rows = pl.ds(pl.multiple_of(p * TILE, TILE), TILE)
        entering = nt3(c_pair, split(s0_ref[rows, :]))
        e = eh[:, tile].astype(F32) + el[:, tile].astype(F32)
        vh, vl = split(x * dx_ref[:, tile] - e * entering)
        za, zb = jnp.concatenate(z[0], axis=1), jnp.concatenate(z[1], axis=1)
        v_ref[p] = (
            nt(picker, vh)
            + nt(picker, vl)
            - jnp.where(sub == 0, za, jnp.where(sub == 1, zb, 0.0))
        )
        return carry

    lax.fori_loop(0, PAIRS, inner, 0)

    table = jnp.where(causal, et[...], 0.0)
    db_ref[...] = nn3(split(table), c_pair)
    s_pair = split(s0_ref[...])
    dc_ref[...] = nn3(split(table.T), b_pair) + nn3((eh[...], el[...]), s_pair)


def run_local(x, ld, b, c, s0, dy):
    vm = pl.BlockSpec(memory_space=pltpu.VMEM)
    shape = jax.ShapeDtypeStruct
    return pl.pallas_call(
        local_kernel,
        out_shape=(
            shape((STATE, ROWS), F32),
            shape((1, ROWS), F32),
            shape((1, TILE), F32),
            shape((TOK, ROWS), F32),
            shape((TOK, ROWS), BF16),
            shape((TOK, ROWS), BF16),
            shape((TOK, ROWS), F32),
            shape((PAIRS, 8, TOK), F32),
            shape((TOK, STATE), F32),
            shape((TOK, STATE), F32),
        ),
        in_specs=[vm] * 6,
        out_specs=(vm,) * 10,
        scratch_shapes=[
            pltpu.VMEM((32, TOK), F32),
            pltpu.VMEM((TOK, HEADS * TILE), F32),
            pltpu.VMEM((HEADS, 1, TOK), F32),
            pltpu.VMEM((TOK, TOK), F32),
            pltpu.VMEM((TOK, TOK), F32),
            pltpu.VMEM((TOK, ROWS), BF16),
            pltpu.VMEM((TOK, ROWS), BF16),
        ],
        compiler_params=pltpu.CompilerParams(vmem_limit_bytes=60 * 1024 * 1024),
        name="local",
    )(x, ld, b, c, s0, dy)


def scan_kernel(
    gt_ref, l3_ref, out_ref,
    pg, pl3, chip, chip_l3, g1, zbuf, zl3, inside, xg, xl, lbuf, back, other,
    pair_s, pair_r, z_s, z_r, x_s, x_r, b_s, b_r,
):
    me, hd = lax.axis_index("seq"), lax.axis_index("head")
    core = lax.rem(me, 2)
    z = lax.rem(me // 2, ZN)
    x = me // (2 * ZN)

    def peer(px, pz, pc):
        return (px * 2 * ZN + pz * 2 + pc, hd)

    mate = peer(x, z, 1 - core)
    z_peers = [lax.rem(z + d, ZN) for d in range(1, ZN)]
    x_peers = [lax.rem(x + d, XN) for d in range(1, XN)]
    barrier = pltpu.get_barrier_semaphore()
    everyone = [mate] + [peer(x, q, core) for q in z_peers] + [peer(q, z, core) for q in x_peers]
    for device in everyone:
        pl.semaphore_signal(barrier, inc=1, device_id=device, device_id_type=MESH)
    pl.semaphore_wait(barrier, len(everyone))

    def send(src, dst, s, r, device):
        copy = pltpu.make_async_remote_copy(
            src_ref=src, dst_ref=dst, send_sem=s, recv_sem=r, device_id=device, device_id_type=MESH
        )
        copy.start()
        return copy

    away = pl.ds(pl.multiple_of((1 - core) * HALF, HALF), HALF)
    mine = pl.ds(pl.multiple_of(core * HALF, HALF), HALF)
    c0 = send(gt_ref.at[away], pg, pair_s.at[0], pair_r.at[0], mate)
    c1 = send(l3_ref, pl3, pair_s.at[1], pair_r.at[1], mate)
    spread = jnp.where(
        (iota((TILE, ROWS), 0) & 31) == (iota((TILE, ROWS), 1) >> 6), 1.0, 0.0
    ).astype(BF16)
    even = core == 0
    c1.wait()
    own_l3, mate_l3 = l3_ref[...], pl3[...]
    l0 = jnp.where(even, own_l3, mate_l3)
    l1 = jnp.where(even, mate_l3, own_l3)
    chip_l3[0] = l0
    chip_l3[1] = l1
    pair_logs = nn(jnp.concatenate([l0, l1], axis=0).astype(BF16), spread)
    a0, a1 = jnp.exp2(pair_logs[0:1]), jnp.exp2(pair_logs[1:2])
    c0.wait()
    for j in range(ZN):
        rows = pl.ds(pl.multiple_of(core * HALF + j * SLICE, SLICE), SLICE)
        part, mate_part = gt_ref[rows, :], pg[j * SLICE : (j + 1) * SLICE, :]
        later = jnp.where(even, mate_part, part)
        g1[j] = later
        chip[j] = jnp.where(even, part, mate_part) + a0 * later
    copies = []
    for q, d in zip(z_peers, range(ZN - 1)):
        device = peer(x, q, core)
        copies.append(send(chip_l3, zl3.at[z], z_s.at[0, d], z_r.at[0, d], device))
        copies.append(send(chip.at[q], zbuf.at[z], z_s.at[1, d], z_r.at[1, d], device))
    zbuf[z] = chip[z]
    zl3[z] = chip_l3[...]
    for copy in copies:
        copy.wait()
    logs = [nn(jnp.concatenate([zl3[j, 0], zl3[j, 1]], axis=0).astype(BF16), spread) for j in range(ZN)]
    logs = [v[0:1] + v[1:2] for v in logs]
    state = jnp.zeros((SLICE, ROWS), F32)
    log = jnp.zeros((1, ROWS), F32)
    factor = [None] * ZN
    for j in reversed(range(ZN)):
        inside[j] = state
        factor[j] = jnp.exp2(log)
        state = zbuf[j] + jnp.exp2(logs[j]) * state
        log = log + logs[j]
    xg[x] = state
    xl[x] = jnp.exp2(log)
    copies = []
    for q, d in zip(x_peers, range(XN - 1)):
        device = peer(q, z, core)
        copies.append(send(xl.at[x], xl.at[x], x_s.at[0, d], x_r.at[0, d], device))
        copies.append(send(xg.at[x], xg.at[x], x_s.at[1, d], x_r.at[1, d], device))
    for copy in copies:
        copy.wait()
    carry = jnp.zeros((SLICE, ROWS), F32)
    for q in reversed(range(1, XN)):
        carry = jnp.where(q > x, xg[q] + xl[q] * carry, carry)
    for j in range(ZN):
        lbuf[j] = inside[j] + factor[j] * carry
    copies = []
    for q, d in zip(z_peers, range(ZN - 1)):
        copies.append(send(lbuf.at[q], back.at[z], b_s.at[d], b_r.at[d], peer(x, q, core)))
    back[z] = lbuf[z]
    for copy in copies:
        copy.wait()
    for j in range(ZN):
        late = back[j]
        early = g1[j] + a1 * late
        rows = pl.ds(pl.multiple_of(core * HALF + j * SLICE, SLICE), SLICE)
        out_ref[rows, :] = jnp.where(even, early, late)
        other[j * SLICE : (j + 1) * SLICE, :] = jnp.where(even, late, early)
    c2 = send(other, out_ref.at[mine], pair_s.at[2], pair_r.at[2], mate)
    c2.wait()


def run_scan(gt, l3):
    vm = pl.BlockSpec(memory_space=pltpu.VMEM)
    dma = pltpu.SemaphoreType.DMA
    slab = pltpu.VMEM((ZN, SLICE, ROWS), F32)
    return pl.pallas_call(
        scan_kernel,
        out_shape=jax.ShapeDtypeStruct((STATE, ROWS), F32),
        in_specs=[vm, vm],
        out_specs=vm,
        scratch_shapes=[
            pltpu.VMEM((HALF, ROWS), F32),
            pltpu.VMEM((1, TILE), F32),
            slab,
            pltpu.VMEM((2, 1, TILE), F32),
            slab,
            slab,
            pltpu.VMEM((ZN, 2, 1, TILE), F32),
            slab,
            pltpu.VMEM((XN, SLICE, ROWS), F32),
            pltpu.VMEM((XN, 1, ROWS), F32),
            slab,
            slab,
            pltpu.VMEM((HALF, ROWS), F32),
            dma((3,)), dma((3,)),
            dma((2, ZN - 1)), dma((2, ZN - 1)),
            dma((2, XN - 1)), dma((2, XN - 1)),
            dma((ZN - 1,)), dma((ZN - 1,)),
        ],
        compiler_params=pltpu.CompilerParams(
            collective_id=0, has_side_effects=True, vmem_limit_bytes=32 * 1024 * 1024
        ),
        name="scan",
    )(gt, l3)


def final_kernel(
    lat_ref, txh_ref, txl_ref, tail_ref, dxl_ref, gt_ref, a_ref, s0_ref, b_ref, v_ref, dbl_ref, dc_ref,
    dx_ref, dld_ref, sum_ref, eg_ref,
    lh, ll, w, g1, own, got,
    r_s, r_r, g_s, g_r,
):
    me, hd = lax.axis_index("seq"), lax.axis_index("head")
    peers = [lax.rem(hd + d, HN) for d in range(1, HN)]
    barrier = pltpu.get_barrier_semaphore()
    for q in peers:
        pl.semaphore_signal(barrier, inc=1, device_id=(me, q), device_id_type=MESH)
    pl.semaphore_wait(barrier, HN - 1)

    hi, lo = split(lat_ref[...])
    lh[...] = hi
    ll[...] = lo
    db = nt3((txh_ref[...], txl_ref[...]), (hi, lo)) + dbl_ref[...]
    part = TOK // HN
    for q in range(HN):
        rows = slice(q * part, (q + 1) * part)
        own[q, :, 0:STATE] = db[rows]
        own[q, :, STATE:] = dc_ref[rows, :]
    copies = []
    for q, d in zip(peers, range(HN - 1)):
        copy = pltpu.make_async_remote_copy(
            src_ref=own.at[q], dst_ref=got.at[d], send_sem=r_s.at[d], recv_sem=r_r.at[d],
            device_id=(me, q), device_id_type=MESH,
        )
        copy.start()
        copies.append(copy)

    b_pair = split(b_ref[...])
    picker = pair_picker()
    sub = iota((8, TILE), 0)

    def correct(p, carry):
        tile = pl.ds(pl.multiple_of(p * TILE, TILE), TILE)
        pair = (lh[:, tile], ll[:, tile])
        raw = nn3(b_pair, pair)
        dx_ref[:, tile] = dxl_ref[:, tile] + tail_ref[:, tile] * raw
        tx = txh_ref[:, tile].astype(F32) + txl_ref[:, tile].astype(F32)
        vh, vl = split(tx * raw)
        w[pl.ds(pl.multiple_of(p * 8, 8), 8), :] = v_ref[p] + nt(picker, vh) + nt(picker, vl)
        eg = (a_ref[:, tile] * lat_ref[:, tile] + gt_ref[:, tile]).T
        rows = pl.ds(pl.multiple_of(p * TILE, TILE), TILE)
        eg_ref[rows, :] = eg
        product = eg * s0_ref[rows, :]
        one = jnp.sum(jnp.sum(product[:WIDTH], axis=0, keepdims=True), axis=1, keepdims=True)
        two = jnp.sum(jnp.sum(product[WIDTH:], axis=0, keepdims=True), axis=1, keepdims=True)
        g1[pl.ds(pl.multiple_of(p * 8, 8), 8), :] = jnp.where(
            sub == 0, one, jnp.where(sub == 1, two, 0.0)
        )
        return carry

    lax.fori_loop(0, PAIRS, correct, 0)
    rates = prefix_sums(w[...], True) + g1[:, 0:1]
    for h in range(HEADS):
        k = (h // 2) * 8 + h % 2
        dld_ref[h : h + 1, :] = rates[k : k + 1, :]

    for copy in copies:
        copy.wait()
    here = pl.ds(pl.multiple_of(hd * part, part), part)
    sum_ref[here, :] = own[hd] + got[0] + got[1] + got[2]
    copies = []
    for q, d in zip(peers, range(HN - 1)):
        copy = pltpu.make_async_remote_copy(
            src_ref=sum_ref.at[here], dst_ref=sum_ref.at[here], send_sem=g_s.at[d], recv_sem=g_r.at[d],
            device_id=(me, q), device_id_type=MESH,
        )
        copy.start()
        copies.append(copy)
    for copy in copies:
        copy.wait()


def run_final(lat, txh, txl, tail, dxl, gt, a, s0, b, v, dbl, dc):
    vm = pl.BlockSpec(memory_space=pltpu.VMEM)
    dma = pltpu.SemaphoreType.DMA
    shape = jax.ShapeDtypeStruct
    return pl.pallas_call(
        final_kernel,
        out_shape=(
            shape((TOK, ROWS), F32),
            shape((HEADS, TOK), F32),
            shape((TOK, 2 * STATE), F32),
            shape((ROWS, STATE), F32),
        ),
        in_specs=[vm] * 12,
        out_specs=(vm,) * 4,
        scratch_shapes=[
            pltpu.VMEM((STATE, ROWS), BF16),
            pltpu.VMEM((STATE, ROWS), BF16),
            pltpu.VMEM((PAIRS * 8, TOK), F32),
            pltpu.VMEM((PAIRS * 8, TILE), F32),
            pltpu.VMEM((HN, TOK // HN, 2 * STATE), F32),
            pltpu.VMEM((HN - 1, TOK // HN, 2 * STATE), F32),
            dma((HN - 1,)), dma((HN - 1,)), dma((HN - 1,)), dma((HN - 1,)),
        ],
        compiler_params=pltpu.CompilerParams(
            collective_id=1, has_side_effects=True, vmem_limit_bytes=60 * 1024 * 1024
        ),
        name="final",
    )(lat, txh, txl, tail, dxl, gt, a, s0, b, v, dbl, dc)


def per_device(inputs, log_decay, b_proj, c_proj, entry_states, out_grad):
    s0 = entry_states.reshape(ROWS, STATE)
    gt, a, l3, dxl, txh, txl, tail, v, dbl, dc = run_local(
        inputs, log_decay, b_proj, c_proj, s0, out_grad
    )
    lat = run_scan(gt, l3)
    dx, dld, total, eg = run_final(lat, txh, txl, tail, dxl, gt, a, s0, b_proj, v, dbl, dc)
    return (dx, dld, total[:, :STATE], total[:, STATE:], eg.reshape(1, HEADS, WIDTH, STATE))


def solution(mesh):
    return jax.shard_map(
        per_device,
        mesh=mesh,
        in_specs=(
            P("seq", "head"),
            P("head", "seq"),
            P("seq", None),
            P("seq", None),
            P("seq", "head", None, None),
            P("seq", "head"),
        ),
        out_specs=(
            P("seq", "head"),
            P("head", "seq"),
            P("seq", None),
            P("seq", None),
            P("seq", "head", None, None),
        ),
        check_vma=False,
    )
```

profile of v0, /device:TPU:16, one launch (start us, length us, event | category | flops | bytes accessed | tf_op | source)
XLA Modules:
  0.0 96.8 jit_solution(1334999327573323530)
XLA Ops:
  0.6 26.0 %local.1 = (f32[128,1280]{1,0:T(8,128)}, f32[1,1280]{1,0:T(1,128)}, f32[1,128]{1,0:T(1,128)}, f32[512,1280]{1,0:T(8,128)}, bf16[512,1280]{1,0:T(8,128)(2,1)}, /*...) custom-call(f32[512,1280]{1,0:T(8,128)} %x_ref.1, ...), custom_call_target="tpu_custom_call" | custom-call | tf_op jit(solution)/shard_map/local/pallas_call | solution.py:216
  26.6 0.0 copy-start
  26.6 1.1 %copy-done = f32[128,1280]{1,0:T(8,128)S(1)} copy-done((f32[128,1280]{1,0:T(8,128)S(1)}, f32[128,1280]{1,0:T(8,128)}, u32[]{:S(2)}) %copy-start) | copy-done | bytes 655384
  27.7 0.0 copy-start.2
  27.7 0.6 copy-done.2
  28.3 35.7 %scan.1.lat_ref = f32[128,1280]{1,0:T(8,128)S(1)} custom-call(f32[128,1280]{1,0:T(8,128)S(1)} %copy-done, f32[1,128]{1,0:T(1,128)S(1)} %copy-done.2), custom_call_target="tpu_custom_call" | custom-call | tf_op jit(solution)/shard_map/scan/pallas_call | solution.py:351
  64.0 0.0 copy-start.1
  64.0 0.9 copy-done.1
  64.9 25.1 %final.1 = (f32[512,1280]{1,0:T(8,128)}, f32[20,512]{1,0:T(8,128)}, f32[512,256]{1,0:T(8,128)}, f32[1280,128]{1,0:T(8,128)}) custom-call(f32[128,1280]{1,0:T(8,128)} %copy-done.1, bf16[512,1280]{1,0:T(8,128)(2,1)} %get-tuple-element.21.txh_ref, bf16[512,1280]{1,0:T(8,128)(2,1)} %get-tuple-element.22.txl_ref, f32[512,1280]{1,0:T(8,128)} %get-tuple-element.23.tail_ref, ...), custom_call_target="tpu_custom_call" | custom-call | tf_op jit(solution)/shard_map/final/pallas_call | solution.py:462
  90.0 1.9 %fusion = (f32[512,128]{1,0:T(8,128)}, f32[512,128]{1,0:T(8,128)}) fusion(f32[512,256]{1,0:T(8,128)} %get-tuple-element.31), kind=kLoop, calls=%fused_computation | loop fusion | bytes 1048576 | tf_op jit(solution)/shard_map/slice | solution.py:495
  91.8 0.0 copy-start.4
  91.8 0.0 copy-start.3
  91.8 3.5 %copy.14 = f32[512,1280]{1,0:T(8,128)} copy(f32[512,1280]{1,0:T(8,128)} %get-tuple-element.40) | data formatting | bytes 5242880
  95.3 0.0 copy-done.4
  95.3 0.6 copy.15
  95.9 0.0 copy-done.3
  95.9 0.8 copy.16
Async XLA Ops:
  26.6 1.1 %copy-start = (f32[128,1280]{1,0:T(8,128)S(1)}, f32[128,1280]{1,0:T(8,128)}, u32[]{:S(2)}) copy-start(f32[128,1280]{1,0:T(8,128)} %get-tuple-element.19.gt_ref) | copy-start | bytes 1966084
  27.7 0.6 copy-start.2
  64.0 0.9 copy-start.1
  91.8 3.5 %copy-start.4 = (f32[20,512]{1,0:T(8,128)S(1)}, f32[20,512]{1,0:T(8,128)}, u32[]{:S(2)}) copy-start(f32[20,512]{1,0:T(8,128)} %get-tuple-element.41) | copy-start | bytes 122884
  91.8 4.1 %copy-start.3 = (f32[1280,128]{1,0:T(8,128)S(1)}, f32[1280,128]{1,0:T(8,128)}, u32[]{:S(2)}) copy-start(f32[1280,128]{1,0:T(8,128)} %get-tuple-element.32) | copy-start | bytes 1966084
where the time goes:
time: 98.4 us; the launch traced here: 96.8 us
  Pallas kernels  86.8 us (88%)
  local copies, waits for them, and re-layouts  9.32 us (9%)
    pallas_call x1, Pallas kernels, run_scan(): pl.pallas_call(scan_kernel, out_shape=jax.ShapeDtypeStruct((STATE, ROWS),...  35.7 us
    pallas_call x1, Pallas kernels, run_local(): pl.pallas_call(local_kernel, out_shape=(shape((STATE, ROWS), F32), shape(...  26 us
    pallas_call x1, Pallas kernels, run_final(): pl.pallas_call(final_kernel, out_shape=(shape((TOK, ROWS), F32), shape((H...  25.1 us
    unnamed x13, local copies, waits for them, and re-layouts  7.47 us

commit v1 on v0

v1 whole, which is shorter than its diff:
```python
import functools

import jax
import jax.numpy as jnp
from jax import lax
from jax.experimental import pallas as pl
from jax.experimental.pallas import tpu as pltpu
from jax.sharding import PartitionSpec as P

F32 = jnp.float32
BF16 = jnp.bfloat16
MESH = pl.DeviceIdType.MESH
TOK = 512
HEADS = 20
WIDTH = 64
STATE = 128
ROWS = HEADS * WIDTH
PAIRS = HEADS // 2
TILE = 128
LOG2E = 1.4426950408889634
ZN = 8
XN = 4
HN = 4
HALF = STATE // 2
SLICE = HALF // ZN
CUT_Z = 4
CUT_X = 6
CUT_Y = 5
VMEM_LIMIT = 58 * 1024 * 1024
OUT = pltpu.VMEM


def split(v):
    hi = v.astype(BF16)
    return hi, (v - hi.astype(F32)).astype(BF16)


def split3(v):
    hi = v.astype(BF16)
    rest = v - hi.astype(F32)
    mid = rest.astype(BF16)
    return hi, mid, (rest - mid.astype(F32)).astype(BF16)


def nn(a, b):
    return lax.dot_general(a, b, (((1,), (0,)), ((), ())), preferred_element_type=F32)


def nt(a, b):
    return lax.dot_general(a, b, (((1,), (1,)), ((), ())), preferred_element_type=F32)


def nn3(a, b):
    a_hi, a_lo = a
    b_hi, b_lo = b
    width = b_hi.shape[1]
    both = nn(a_hi, jnp.concatenate([b_hi, b_lo], axis=1))
    return both[:, :width] + both[:, width:] + nn(a_lo, b_hi)


def nt3(a, b):
    a_hi, a_lo = a
    b_hi, b_lo = b
    return nt(a_hi, b_hi) + nt(a_hi, b_lo) + nt(a_lo, b_hi)


def iota(shape, dim):
    return lax.broadcasted_iota(jnp.int32, shape, dim)


def prefix_sums(value, strict):
    rows = value.shape[0]
    a, b = iota((TILE, TILE), 0), iota((TILE, TILE), 1)
    upper = jnp.where(a < b if strict else a <= b, 1.0, 0.0).astype(BF16)
    tiles = []
    base = jnp.zeros((rows, 1), F32)
    for j in range(TOK // TILE):
        part = value[:, j * TILE : (j + 1) * TILE]
        hi, mid, lo = split3(part)
        inner = nn(hi, upper) + nn(mid, upper) + nn(lo, upper)
        tiles.append(inner + base)
        last = tiles[-1][:, TILE - 1 : TILE]
        base = last + part[:, TILE - 1 : TILE] if strict else last
    return jnp.concatenate(tiles, axis=1)


def pair_picker():
    row, lane = iota((8, TILE), 0), iota((8, TILE), 1)
    low = (row == 0) & (lane < WIDTH)
    high = (row == 1) & (lane >= WIDTH)
    return jnp.where(low | high, 1.0, 0.0).astype(BF16)


def main_kernel(
    x_hbm, ld_ref, b_ref, c_ref, s0_hbm, dy_hbm,
    dx_ref, dld_ref, db_ref, dc_ref, eg_ref,
    x_ref, s0_ref, dy_ref, gt_ref, a_ref, txh, txl, tail_ref, v_ref, dbl,
    ld32, lx, lrow, cbt, et, eh, el,
    l3, pg, pl3, chip, chip_l3, g1, zbuf, zl3, inside, fac, xg, xl, lbuf, back, other, lat,
    lh, ll, w, first_g, own_c, got_c, own_b, got_b,
    in_s, pair_s, pair_r, z_s, z_r, x_s, x_r, b_s, b_r, y_s, y_r,
):
    me, hd = lax.axis_index("seq"), lax.axis_index("head")
    core = lax.rem(me, 2)
    z = lax.rem(me // 2, ZN)
    x = me // (2 * ZN)
    even = core == 0

    def peer(px, pz, pc):
        return (px * 2 * ZN + pz * 2 + pc, hd)

    mate = peer(x, z, 1 - core)
    z_peers = [lax.rem(z + d, ZN) for d in range(1, ZN)]
    x_peers = [lax.rem(x + d, XN) for d in range(1, XN)]
    y_peers = [lax.rem(hd + d, HN) for d in range(1, HN)]
    barrier = pltpu.get_barrier_semaphore()
    everyone = (
        [mate]
        + [peer(x, q, core) for q in z_peers]
        + [peer(q, z, core) for q in x_peers]
        + [(me, q) for q in y_peers]
    )
    for device in everyone:
        pl.semaphore_signal(barrier, inc=1, device_id=device, device_id_type=MESH)
    loads = [
        pltpu.make_async_copy(dy_hbm, dy_ref, in_s.at[0]),
        pltpu.make_async_copy(x_hbm, x_ref, in_s.at[1]),
        pltpu.make_async_copy(s0_hbm, s0_ref, in_s.at[2]),
    ]
    for load in loads:
        load.start()

    def send(src, dst, s, r, device):
        copy = pltpu.make_async_remote_copy(
            src_ref=src, dst_ref=dst, send_sem=s, recv_sem=r, device_id=device, device_id_type=MESH
        )
        copy.start()
        return copy

    first = iota((1, TILE), 1) < WIDTH
    ld32[...] = jnp.zeros_like(ld32)
    ld32[0:HEADS, :] = ld_ref[...] * LOG2E
    cum = prefix_sums(ld32[...], False)
    for h in range(HEADS):
        lrow[h] = cum[h : h + 1, :]
    hi, mid, lo = split3(cum)
    stack = jnp.concatenate(
        [hi.astype(F32), mid.astype(F32), lo.astype(F32), jnp.zeros_like(cum)], axis=0
    )
    columns = stack.T
    l3[...] = columns[TOK - 1 : TOK, :]
    columns = columns.astype(BF16)
    wide = (TILE, HEADS * TILE)
    spread = jnp.where((iota(wide, 0) & 31) == (iota(wide, 1) >> 7), 1.0, 0.0).astype(BF16)
    for k in range(HEADS // 4):
        part = slice(k * 4 * TILE, (k + 1) * 4 * TILE)
        lx[:, part] = nn(columns, spread[:, part])
    ct_pair = split(c_ref[...].T)
    loads[0].wait()

    def tile_of(p):
        return pl.ds(pl.multiple_of(p * TILE, TILE), TILE)

    def logs_of(p):
        la = lx[:, pl.ds(pl.multiple_of(p * 2 * TILE, TILE), TILE)]
        lb = lx[:, pl.ds(pl.multiple_of(p * 2 * TILE + TILE, TILE), TILE)]
        return jnp.where(first, la, lb)

    def start(p, carry):
        tile = tile_of(p)
        both = logs_of(p)
        e_pair = split(jnp.exp2(both) * dy_ref[:, tile])
        eh[:, tile] = e_pair[0]
        el[:, tile] = e_pair[1]
        gt_ref[:, tile] = nn3(ct_pair, e_pair)
        return carry

    lax.fori_loop(0, PAIRS, start, 0)

    pl.semaphore_wait(barrier, len(everyone))
    away = pl.ds(pl.multiple_of((1 - core) * HALF, HALF), HALF)
    mine = pl.ds(pl.multiple_of(core * HALF, HALF), HALF)
    c1 = send(l3, pl3, pair_s.at[1], pair_r.at[1], mate)
    c0 = send(gt_ref.at[away], pg, pair_s.at[0], pair_r.at[0], mate)

    c_pair = split(c_ref[...])
    b_pair = split(b_ref[...])
    causal = iota((TOK, TOK), 0) <= iota((TOK, TOK), 1)
    cbt[...] = jnp.where(causal, nt3(b_pair, c_pair), 0.0)
    et[...] = jnp.zeros_like(et)

    narrow = (TILE, ROWS)
    spread = jnp.where((iota(narrow, 0) & 31) == (iota(narrow, 1) >> 6), 1.0, 0.0).astype(BF16)
    c1.wait()
    own_l3, mate_l3 = l3[...], pl3[...]
    l0 = jnp.where(even, own_l3, mate_l3)
    l1 = jnp.where(even, mate_l3, own_l3)
    chip_l3[0] = l0
    chip_l3[1] = l1
    pair_logs = nn(jnp.concatenate([l0, l1], axis=0).astype(BF16), spread)
    a0, a1 = jnp.exp2(pair_logs[0:1]), jnp.exp2(pair_logs[1:2])
    a_ref[...] = jnp.where(even, a0, a1)
    c0.wait()
    for j in range(ZN):
        rows = pl.ds(pl.multiple_of(core * HALF + j * SLICE, SLICE), SLICE)
        part, mate_part = gt_ref[rows, :], pg[j * SLICE : (j + 1) * SLICE, :]
        later = jnp.where(even, mate_part, part)
        g1[j] = later
        chip[j] = jnp.where(even, part, mate_part) + a0 * later
    z_copies = []
    for q, d in zip(z_peers, range(ZN - 1)):
        device = peer(x, q, core)
        z_copies.append(send(chip_l3, zl3.at[z], z_s.at[0, d], z_r.at[0, d], device))
        z_copies.append(send(chip.at[q], zbuf.at[z], z_s.at[1, d], z_r.at[1, d], device))
    zbuf[z] = chip[z]
    zl3[z] = chip_l3[...]

    picker = pair_picker()
    sub = iota((8, TOK), 0)

    def inner(p, carry):
        tile = tile_of(p)
        xv, dy = x_ref[:, tile], dy_ref[:, tile]
        both = logs_of(p)
        tail = jnp.exp2(both[TOK - 1 : TOK, :] - both)
        tail_ref[:, tile] = tail
        tx = split(tail * xv)
        txh[:, tile] = tx[0]
        txl[:, tile] = tx[1]
        xh, xlo = split(xv)
        dyh, dyl = split(dy)
        xh_f, dyh_f = xh.astype(F32), dyh.astype(F32)
        x_turn = pltpu.roll(xlo.astype(F32), WIDTH, 1)
        dy_turn = pltpu.roll(dyh_f, WIDTH, 1)
        dyl_f = dyl.astype(F32)
        zero = jnp.zeros_like(xv)
        dycat = jnp.concatenate([dyh, dyl], axis=1)
        left, right = [], []
        for k in range(2):
            here = first if k == 0 else jnp.logical_not(first)
            left.append(
                jnp.concatenate(
                    [jnp.where(here, xh_f, x_turn), jnp.where(here, xh_f, zero)], axis=1
                ).astype(BF16)
            )
            right.append(
                jnp.concatenate(
                    [jnp.where(here, dyh_f, dy_turn), jnp.where(here, dyl_f, zero)], axis=1
                ).astype(BF16)
            )
        zs = [[jnp.zeros((1, TILE), F32) for j in range(4)] for k in range(2)]
        for i in range(4):
            r = i * TILE
            mix = cbt[r : r + TILE, r:]
            outs = []
            gained = et[r : r + TILE, r:]
            for k in range(2):
                grad = nt(left[k][r : r + TILE], right[k][r:])
                column = lx[r : r + TILE, pl.ds(pl.multiple_of((2 * p + k) * TILE, TILE), TILE)]
                row = lrow[2 * p + k][:, r:]
                decay = []
                for j in range(4 - i):
                    gap = row[:, j * TILE : (j + 1) * TILE] - column
                    decay.append(jnp.exp2(jnp.minimum(gap, 0.0) if j == 0 else gap))
                decay = jnp.concatenate(decay, axis=1)
                weight = decay * mix
                gained = gained + decay * grad
                sums = jnp.sum(weight * grad, axis=0, keepdims=True)
                for j in range(4 - i):
                    zs[k][i + j] = zs[k][i + j] + sums[:, j * TILE : (j + 1) * TILE]
                wh, wl = split(weight)
                out = nn(wh, dycat[r:])
                outs.append(out[:, :TILE] + out[:, TILE:] + nn(wl, dyh[r:]))
            et[r : r + TILE, r:] = gained
            dx_ref[r : r + TILE, tile] = jnp.where(first, outs[0], outs[1])
        entering = nt3(c_pair, split(s0_ref[tile, :]))
        e = eh[:, tile].astype(F32) + el[:, tile].astype(F32)
        vh, vl = split(xv * dx_ref[:, tile] - e * entering)
        za, zb = jnp.concatenate(zs[0], axis=1), jnp.concatenate(zs[1], axis=1)
        v_ref[p] = (
            nt(picker, vh)
            + nt(picker, vl)
            - jnp.where(sub == 0, za, jnp.where(sub == 1, zb, 0.0))
        )
        return carry

    loads[1].wait()
    loads[2].wait()
    lax.fori_loop(0, CUT_Z, inner, 0)

    for copy in z_copies:
        copy.wait()
    logs = [nn(jnp.concatenate([zl3[j, 0], zl3[j, 1]], axis=0).astype(BF16), spread) for j in range(ZN)]
    logs = [v[0:1] + v[1:2] for v in logs]
    state = jnp.zeros((SLICE, ROWS), F32)
    log = jnp.zeros((1, ROWS), F32)
    for j in reversed(range(ZN)):
        inside[j] = state
        fac[j] = jnp.exp2(log)
        state = zbuf[j] + jnp.exp2(logs[j]) * state
        log = log + logs[j]
    xg[x] = state
    xl[x] = jnp.exp2(log)
    x_copies = []
    for q, d in zip(x_peers, range(XN - 1)):
        device = peer(q, z, core)
        x_copies.append(send(xl.at[x], xl.at[x], x_s.at[0, d], x_r.at[0, d], device))
        x_copies.append(send(xg.at[x], xg.at[x], x_s.at[1, d], x_r.at[1, d], device))

    lax.fori_loop(CUT_Z, CUT_X, inner, 0)

    for copy in x_copies:
        copy.wait()
    entering = jnp.zeros((SLICE, ROWS), F32)
    for q in reversed(range(1, XN)):
        entering = jnp.where(q > x, xg[q] + xl[q] * entering, entering)
    for j in range(ZN):
        lbuf[j] = inside[j] + fac[j] * entering
    b_copies = []
    for q, d in zip(z_peers, range(ZN - 1)):
        b_copies.append(send(lbuf.at[q], back.at[z], b_s.at[d], b_r.at[d], peer(x, q, core)))
    back[z] = lbuf[z]

    lax.fori_loop(CUT_X, PAIRS, inner, 0)

    part = TOK // HN
    here = pl.ds(pl.multiple_of(hd * part, part), part)

    def scatter(own, got, k):
        return [
            send(own.at[q], got.at[d], y_s.at[k, d], y_r.at[k, d], (me, q))
            for q, d in zip(y_peers, range(HN - 1))
        ]

    def gather(own, got, out, k):
        out[here, :] = own[hd] + got[0] + got[1] + got[2]
        return [
            send(out.at[here], out.at[here], y_s.at[k, d], y_r.at[k, d], (me, q))
            for q, d in zip(y_peers, range(HN - 1))
        ]

    table = jnp.where(causal, et[...], 0.0)
    s_pair = split(s0_ref[...])
    dc = nn3(split(table.T), b_pair) + nn3((eh[...], el[...]), s_pair)
    for q in range(HN):
        own_c[q] = dc[q * part : (q + 1) * part]
    c_copies = scatter(own_c, got_c, 0)
    dbl[...] = nn3(split(table), c_pair)

    for copy in b_copies:
        copy.wait()
    for j in range(ZN):
        late = back[j]
        early = g1[j] + a1 * late
        rows = pl.ds(pl.multiple_of(core * HALF + j * SLICE, SLICE), SLICE)
        lat[rows, :] = jnp.where(even, early, late)
        other[j * SLICE : (j + 1) * SLICE, :] = jnp.where(even, late, early)
    c2 = send(other, lat.at[mine], pair_s.at[2], pair_r.at[2], mate)
    for copy in c_copies:
        copy.wait()
    c_copies = gather(own_c, got_c, dc_ref, 1)
    c2.wait()

    hi, lo = split(lat[...])
    lh[...] = hi
    ll[...] = lo
    db = nt3((txh[...], txl[...]), (hi, lo)) + dbl[...]
    for q in range(HN):
        own_b[q] = db[q * part : (q + 1) * part]
    d_copies = scatter(own_b, got_b, 2)

    top = iota((8, TILE), 0)

    def correct(p, carry):
        tile = tile_of(p)
        raw = nn3(b_pair, (lh[:, tile], ll[:, tile]))
        dx_ref[:, tile] = dx_ref[:, tile] + tail_ref[:, tile] * raw
        tx = txh[:, tile].astype(F32) + txl[:, tile].astype(F32)
        vh, vl = split(tx * raw)
        w[pl.ds(pl.multiple_of(p * 8, 8), 8), :] = v_ref[p] + nt(picker, vh) + nt(picker, vl)
        eg = (a_ref[:, tile] * lat[:, tile] + gt_ref[:, tile]).T
        eg_ref[tile, :] = eg
        product = eg * s0_ref[tile, :]
        one = jnp.sum(jnp.sum(product[:WIDTH], axis=0, keepdims=True), axis=1, keepdims=True)
        two = jnp.sum(jnp.sum(product[WIDTH:], axis=0, keepdims=True), axis=1, keepdims=True)
        first_g[pl.ds(pl.multiple_of(p * 8, 8), 8), :] = jnp.where(
            top == 0, one, jnp.where(top == 1, two, 0.0)
        )
        return carry

    lax.fori_loop(0, CUT_Y, correct, 0)
    for copy in d_copies:
        copy.wait()
    d_copies = gather(own_b, got_b, db_ref, 3)
    lax.fori_loop(CUT_Y, PAIRS, correct, 0)
    rates = prefix_sums(w[...], True) + first_g[:, 0:1]
    for h in range(HEADS):
        k = (h // 2) * 8 + h % 2
        dld_ref[h : h + 1, :] = rates[k : k + 1, :]
    for copy in c_copies:
        copy.wait()
    for copy in d_copies:
        copy.wait()


def run(x, ld, b, c, s0, dy):
    vm = pl.BlockSpec(memory_space=pltpu.VMEM)
    hbm = pl.BlockSpec(memory_space=pltpu.HBM)
    dma = pltpu.SemaphoreType.DMA
    shape = jax.ShapeDtypeStruct
    slab = pltpu.VMEM((ZN, SLICE, ROWS), F32)
    tall = pltpu.VMEM((TOK, ROWS), F32)
    tall16 = pltpu.VMEM((TOK, ROWS), BF16)
    state = pltpu.VMEM((STATE, ROWS), F32)
    quarter = TOK // HN
    return pl.pallas_call(
        main_kernel,
        out_shape=(
            OUT((TOK, ROWS), F32),
            OUT((HEADS, TOK), F32),
            OUT((TOK, STATE), F32),
            OUT((TOK, STATE), F32),
            OUT((ROWS, STATE), F32),
        ),
        in_specs=[hbm, vm, vm, vm, hbm, hbm],
        out_specs=(vm,) * 5,
        scratch_shapes=[
            tall,
            pltpu.VMEM((ROWS, STATE), F32),
            tall,
            state,
            pltpu.VMEM((1, ROWS), F32),
            tall16,
            tall16,
            tall,
            pltpu.VMEM((PAIRS, 8, TOK), F32),
            pltpu.VMEM((TOK, STATE), F32),
            pltpu.VMEM((32, TOK), F32),
            pltpu.VMEM((TOK, HEADS * TILE), F32),
            pltpu.VMEM((HEADS, 1, TOK), F32),
            pltpu.VMEM((TOK, TOK), F32),
            pltpu.VMEM((TOK, TOK), F32),
            tall16,
            tall16,
            pltpu.VMEM((1, TILE), F32),
            pltpu.VMEM((HALF, ROWS), F32),
            pltpu.VMEM((1, TILE), F32),
            slab,
            pltpu.VMEM((2, 1, TILE), F32),
            slab,
            slab,
            pltpu.VMEM((ZN, 2, 1, TILE), F32),
            slab,
            pltpu.VMEM((ZN, 1, ROWS), F32),
            pltpu.VMEM((XN, SLICE, ROWS), F32),
            pltpu.VMEM((XN, 1, ROWS), F32),
            slab,
            slab,
            pltpu.VMEM((HALF, ROWS), F32),
            state,
            pltpu.VMEM((STATE, ROWS), BF16),
            pltpu.VMEM((STATE, ROWS), BF16),
            pltpu.VMEM((PAIRS * 8, TOK), F32),
            pltpu.VMEM((PAIRS * 8, TILE), F32),
            pltpu.VMEM((HN, quarter, STATE), F32),
            pltpu.VMEM((HN - 1, quarter, STATE), F32),
            pltpu.VMEM((HN, quarter, STATE), F32),
            pltpu.VMEM((HN - 1, quarter, STATE), F32),
            dma((3,)),
            dma((3,)), dma((3,)),
            dma((2, ZN - 1)), dma((2, ZN - 1)),
            dma((2, XN - 1)), dma((2, XN - 1)),
            dma((ZN - 1,)), dma((ZN - 1,)),
            dma((4, HN - 1)), dma((4, HN - 1)),
        ],
        compiler_params=pltpu.CompilerParams(
            collective_id=0, has_side_effects=True, vmem_limit_bytes=VMEM_LIMIT
        ),
        name="main",
    )(x, ld, b, c, s0, dy)


def per_device(inputs, log_decay, b_proj, c_proj, entry_states, out_grad):
    s0 = entry_states.reshape(ROWS, STATE)
    dx, dld, db, dc, eg = run(inputs, log_decay, b_proj, c_proj, s0, out_grad)
    return (dx, dld, db, dc, eg.reshape(1, HEADS, WIDTH, STATE))


def solution(mesh):
    return jax.shard_map(
        per_device,
        mesh=mesh,
        in_specs=(
            P("seq", "head"),
            P("head", "seq"),
            P("seq", None),
            P("seq", None),
            P("seq", "head", None, None),
            P("seq", "head"),
        ),
        out_specs=(
            P("seq", "head"),
            P("head", "seq"),
            P("seq", None),
            P("seq", None),
            P("seq", "head", None, None),
        ),
        check_vma=False,
    )
```

time: 98.4 us -> 61.7 us (0.63); the launches traced: 96.8 us -> 61.6 us
  Pallas kernels: 86.8 us -> 56.6 us
  local copies, waits for them, and re-layouts: 9.32 us -> 4.35 us
    pallas_call x3 -> x1, Pallas kernels: 86.8 us -> 56.6 us  [run(): pl.pallas_call(main_kernel, out_shape=(OUT((TOK, ROWS), F32), OUT((HEADS,...]
    unnamed x13 -> x5, local copies, waits for them, and re-layouts: 7.47 us -> 4.35 us
    slice x1 -> x0, local copies, waits for them, and re-layouts: 1.85 us -> none  [per_device(): total[:, STATE:]]
where the time goes in v1:
time: 61.7 us; the launch traced here: 61.6 us
  Pallas kernels  56.6 us (92%)
  local copies, waits for them, and re-layouts  4.35 us (7%)
  between operations  0.64 us (1%)
    pallas_call x1, Pallas kernels, run(): pl.pallas_call(main_kernel, out_shape=(OUT((TOK, ROWS), F32), OUT((HEADS,...  56.6 us
    unnamed x5, local copies, waits for them, and re-layouts  4.35 us

profile of v1, /device:TPU:16, one launch (start us, length us, event | category | flops | bytes accessed | tf_op | source)
XLA Modules:
  0.0 61.6 jit_solution(1338186175682467398)
XLA Ops:
  0.6 56.6 %main.1 = (f32[512,1280]{1,0:T(8,128)S(1)}, f32[20,512]{1,0:T(8,128)S(1)}, f32[512,128]{1,0:T(8,128)S(1)}, f32[512,128]{1,0:T(8,128)S(1)}, f32[1280,128]{1,0:T(8,128)S(1)}) custom-call(f32[512,1280]{1,0:T(8,128)} %x_hbm.1, f32[20,512]{1,0:T(8,128)} %ld_ref.1, f32[512,128]{1,0:T(8,128)} %b_ref.1, f32[512,128]{1,0:T(8,128)} %c_ref.1, f32[1280,128]{1,0:T(8,128)} %bitcast.3, ...), custom_call_target="tpu_custom_call" | custom-call | tf_op jit(solution)/shard_map/main/pallas_call | solution.py:416
  57.2 1.5 %copy.16 = f32[512,1280]{1,0:T(8,128)} copy(f32[512,1280]{1,0:T(8,128)S(1)} %get-tuple-element.15) | data formatting | bytes 5242880
  58.7 0.6 %copy.17 = f32[20,512]{1,0:T(8,128)} copy(f32[20,512]{1,0:T(8,128)S(1)} %get-tuple-element.16) | data formatting | bytes 81920
  59.3 0.7 %copy.18 = f32[512,128]{1,0:T(8,128)} copy(f32[512,128]{1,0:T(8,128)S(1)} %get-tuple-element.17) | data formatting | bytes 524288
  60.0 0.7 %copy.19 = f32[512,128]{1,0:T(8,128)} copy(f32[512,128]{1,0:T(8,128)S(1)} %get-tuple-element.18) | data formatting | bytes 524288
  60.7 0.8 %copy.20 = f32[1,20,64,128]{3,2,1,0:T(8,128)} copy(f32[1,20,64,128]{3,2,1,0:T(8,128)S(1)} %bitcast.2) | data formatting | bytes 1310720

commit v2 on v1

v2 whole, which is shorter than its diff:
```python
import functools

import jax
import jax.numpy as jnp
from jax import lax
from jax.experimental import pallas as pl
from jax.experimental.pallas import tpu as pltpu
from jax.sharding import PartitionSpec as P

F32 = jnp.float32
BF16 = jnp.bfloat16
MESH = pl.DeviceIdType.MESH
TOK = 512
HEADS = 20
WIDTH = 64
STATE = 128
ROWS = HEADS * WIDTH
PAIRS = HEADS // 2
TILE = 128
LOG2E = 1.4426950408889634
ZN = 8
XN = 4
HN = 4
HALF = STATE // 2
SLICE = HALF // ZN
LINE = 2 * ZN
PARTS = 2
PART_PAIRS = PAIRS // PARTS
PART = PART_PAIRS * TILE
CUTS = (4, 7, 7, 10)
VMEM_LIMIT = 58 * 1024 * 1024


def split(v):
    hi = v.astype(BF16)
    return hi, (v - hi.astype(F32)).astype(BF16)


def split3(v):
    hi = v.astype(BF16)
    rest = v - hi.astype(F32)
    mid = rest.astype(BF16)
    return hi, mid, (rest - mid.astype(F32)).astype(BF16)


def nn(a, b):
    return lax.dot_general(a, b, (((1,), (0,)), ((), ())), preferred_element_type=F32)


def nt(a, b):
    return lax.dot_general(a, b, (((1,), (1,)), ((), ())), preferred_element_type=F32)


def nn3(a, b):
    a_hi, a_lo = a
    b_hi, b_lo = b
    width = b_hi.shape[1]
    both = nn(a_hi, jnp.concatenate([b_hi, b_lo], axis=1))
    return both[:, :width] + both[:, width:] + nn(a_lo, b_hi)


def nt3(a, b):
    a_hi, a_lo = a
    b_hi, b_lo = b
    return nt(a_hi, b_hi) + nt(a_hi, b_lo) + nt(a_lo, b_hi)


def iota(shape, dim):
    return lax.broadcasted_iota(jnp.int32, shape, dim)


def prefix_sums(value, strict):
    rows = value.shape[0]
    a, b = iota((TILE, TILE), 0), iota((TILE, TILE), 1)
    upper = jnp.where(a < b if strict else a <= b, 1.0, 0.0).astype(BF16)
    tiles = []
    base = jnp.zeros((rows, 1), F32)
    for j in range(TOK // TILE):
        part = value[:, j * TILE : (j + 1) * TILE]
        hi, mid, lo = split3(part)
        inner = nn(hi, upper) + nn(mid, upper) + nn(lo, upper)
        tiles.append(inner + base)
        last = tiles[-1][:, TILE - 1 : TILE]
        base = last + part[:, TILE - 1 : TILE] if strict else last
    return jnp.concatenate(tiles, axis=1)


def pair_picker():
    row, lane = iota((8, TILE), 0), iota((8, TILE), 1)
    low = (row == 0) & (lane < WIDTH)
    high = (row == 1) & (lane >= WIDTH)
    return jnp.where(low | high, 1.0, 0.0).astype(BF16)


def main_kernel(
    x_hbm, ld_hbm, b_hbm, c_hbm, s0_hbm, dy_hbm,
    dx_ref, dld_ref, db_ref, dc_ref, eg_ref,
    x_ref, s0_ref, dy_ref, gt_ref, a_ref, txh, txl, tail_ref, v_ref, dbl,
    ld_ref, b_ref, c_ref, ld32, lanes, lx, lrow, cbt, et, eh, el,
    pg, chip, g1, zbuf, zl3, zrow, inside, fac, step, xg, xl, lbuf, back, other, lat,
    lh, ll, w, first_g, own_c, got_c, own_b, got_b,
    in_s, pair_s, pair_r, l_s, l_r, z_s, z_r, x_s, x_r, b_s, b_r, y_s, y_r,
):
    me, hd = lax.axis_index("seq"), lax.axis_index("head")
    core = lax.rem(me, 2)
    z = lax.rem(me // 2, ZN)
    x = me // (2 * ZN)
    even = core == 0

    def peer(px, pz, pc):
        return (px * 2 * ZN + pz * 2 + pc, hd)

    mate = peer(x, z, 1 - core)
    spot = z * 2 + core
    line = [lax.rem(spot + d, LINE) for d in range(1, LINE)]
    z_peers = [lax.rem(z + d, ZN) for d in range(1, ZN)]
    x_peers = [lax.rem(x + d, XN) for d in range(1, XN)]
    y_peers = [lax.rem(hd + d, HN) for d in range(1, HN)]
    barrier = pltpu.get_barrier_semaphore()
    everyone = (
        [peer(x, q // 2, lax.rem(q, 2)) for q in line]
        + [peer(q, z, core) for q in x_peers]
        + [(me, q) for q in y_peers]
    )

    def lanes_of(k):
        return slice(k * PART, (k + 1) * PART)

    smalls = [
        pltpu.make_async_copy(ld_hbm, ld_ref, in_s.at[PARTS + 2]),
        pltpu.make_async_copy(c_hbm, c_ref, in_s.at[PARTS + 3]),
        pltpu.make_async_copy(b_hbm, b_ref, in_s.at[PARTS + 4]),
    ]
    loads = [
        pltpu.make_async_copy(dy_hbm.at[:, lanes_of(k)], dy_ref.at[:, lanes_of(k)], in_s.at[k])
        for k in range(PARTS)
    ]
    smalls[0].start()
    smalls[1].start()
    for load in loads:
        load.start()
    smalls[2].start()
    for device in everyone:
        pl.semaphore_signal(barrier, inc=1, device_id=device, device_id_type=MESH)
    def send(src, dst, s, r, device):
        copy = pltpu.make_async_remote_copy(
            src_ref=src, dst_ref=dst, send_sem=s, recv_sem=r, device_id=device, device_id_type=MESH
        )
        copy.start()
        return copy

    first = iota((1, TILE), 1) < WIDTH
    smalls[0].wait()
    ld32[...] = jnp.zeros_like(ld32)
    ld32[0:HEADS, :] = ld_ref[...] * LOG2E
    cum = prefix_sums(ld32[...], False)
    for h in range(HEADS):
        lrow[h] = cum[h : h + 1, :]
    hi, mid, lo = split3(cum)
    stack = jnp.concatenate(
        [hi.astype(F32), mid.astype(F32), lo.astype(F32), jnp.zeros_like(cum)], axis=0
    )
    columns = stack.T
    zl3[spot] = columns[TOK - 1 : TOK, :]
    columns = columns.astype(BF16)
    pl.semaphore_wait(barrier, len(everyone))
    l_copies = [
        send(zl3.at[spot], zl3.at[spot], l_s.at[d], l_r.at[d], peer(x, q // 2, lax.rem(q, 2)))
        for q, d in zip(line, range(LINE - 1))
    ]
    narrow = (TILE, ROWS)
    spread = jnp.where((iota(narrow, 0) & 31) == (iota(narrow, 1) >> 6), 1.0, 0.0).astype(BF16)
    lanes[...] = spread
    smalls[1].wait()
    ct_pair = split(c_ref[...].T)

    def tile_of(p):
        return pl.ds(pl.multiple_of(p * TILE, TILE), TILE)

    def logs_of(p):
        return nn(columns, lanes[:, tile_of(p)])

    def starter(k):
        def start(p, carry):
            tile = tile_of(p + k * PART_PAIRS)
            e_pair = split(jnp.exp2(logs_of(p + k * PART_PAIRS)) * dy_ref[:, tile])
            eh[:, tile] = e_pair[0]
            el[:, tile] = e_pair[1]
            gt_ref[k, :, tile_of(p)] = nn3(ct_pair, e_pair)
            return carry

        return start

    away = pl.ds(pl.multiple_of((1 - core) * HALF, HALF), HALF)
    mine = pl.ds(pl.multiple_of(core * HALF, HALF), HALF)
    m_copies = []
    for k in range(PARTS):
        loads[k].wait()
        lax.fori_loop(0, PART_PAIRS, starter(k), 0)
        m_copies.append(send(gt_ref.at[k, away], pg.at[k], pair_s.at[0, k], pair_r.at[0, k], mate))
    rest = [
        pltpu.make_async_copy(x_hbm, x_ref, in_s.at[PARTS]),
        pltpu.make_async_copy(s0_hbm, s0_ref, in_s.at[PARTS + 1]),
    ]
    for load in rest:
        load.start()

    for copy in l_copies:
        copy.wait()
    line_logs = nn(jnp.concatenate([zl3[i] for i in range(LINE)], axis=0).astype(BF16), spread)
    log = jnp.zeros((1, ROWS), F32)
    for j in reversed(range(ZN)):
        one, two = line_logs[2 * j : 2 * j + 1], line_logs[2 * j + 1 : 2 * j + 2]
        zrow[2 * j] = one
        zrow[2 * j + 1] = two
        fac[j] = jnp.exp2(log)
        step[j] = jnp.exp2(one + two)
        log = log + (one + two)
    xl[x] = jnp.exp2(log)
    r_copies = [
        send(xl.at[x], xl.at[x], x_s.at[PARTS, d], x_r.at[PARTS, d], peer(q, z, core))
        for q, d in zip(x_peers, range(XN - 1))
    ]
    a0, a1 = jnp.exp2(zrow[2 * z]), jnp.exp2(zrow[2 * z + 1])
    a_ref[...] = jnp.where(even, a0, a1)

    z_copies = []
    for k in range(PARTS):
        m_copies[k].wait()
        for j in range(ZN):
            rows = pl.ds(pl.multiple_of(core * HALF + j * SLICE, SLICE), SLICE)
            part, mate_part = gt_ref[k, rows, :], pg[k, j * SLICE : (j + 1) * SLICE, :]
            later = jnp.where(even, mate_part, part)
            g1[k, j] = later
            chip[k, j] = jnp.where(even, part, mate_part) + a0[:, lanes_of(k)] * later
        z_copies.append(
            [
                send(chip.at[k, q], zbuf.at[k, z], z_s.at[k, d], z_r.at[k, d], peer(x, q, core))
                for q, d in zip(z_peers, range(ZN - 1))
            ]
        )
        zbuf[k, z] = chip[k, z]

    wide = (TILE, HEADS * TILE)
    spread = jnp.where((iota(wide, 0) & 31) == (iota(wide, 1) >> 7), 1.0, 0.0).astype(BF16)
    for k in range(HEADS // 4):
        part = slice(k * 4 * TILE, (k + 1) * 4 * TILE)
        lx[:, part] = nn(columns, spread[:, part])
    c_pair = split(c_ref[...])
    smalls[2].wait()
    b_pair = split(b_ref[...])
    causal = iota((TOK, TOK), 0) <= iota((TOK, TOK), 1)
    cbt[...] = jnp.where(causal, nt3(b_pair, c_pair), 0.0)
    et[...] = jnp.zeros_like(et)

    picker = jnp.concatenate([pair_picker()] * 2, axis=1)
    c_both = jnp.concatenate(c_pair, axis=1)
    b_both = jnp.concatenate(b_pair, axis=1)
    sub = iota((8, TOK), 0)

    def inner(p, carry):
        tile = tile_of(p)
        xv, dy = x_ref[:, tile], dy_ref[:, tile]
        both = logs_of(p)
        tail = jnp.exp2(both[TOK - 1 : TOK, :] - both)
        tail_ref[:, tile] = tail
        tx = split(tail * xv)
        txh[:, tile] = tx[0]
        txl[:, tile] = tx[1]
        xh, xlo = split(xv)
        dyh, dyl = split(dy)
        xh_f, dyh_f = xh.astype(F32), dyh.astype(F32)
        x_turn = pltpu.roll(xlo.astype(F32), WIDTH, 1)
        dy_turn = pltpu.roll(dyh_f, WIDTH, 1)
        dyl_f = dyl.astype(F32)
        zero = jnp.zeros_like(xv)
        dycat = jnp.concatenate([dyh, dyl], axis=1)
        left, right = [], []
        for k in range(2):
            here = first if k == 0 else jnp.logical_not(first)
            left.append(
                jnp.concatenate(
                    [jnp.where(here, xh_f, x_turn), jnp.where(here, xh_f, zero)], axis=1
                ).astype(BF16)
            )
            right.append(
                jnp.concatenate(
                    [jnp.where(here, dyh_f, dy_turn), jnp.where(here, dyl_f, zero)], axis=1
                ).astype(BF16)
            )
        zs = [[jnp.zeros((1, TILE), F32) for j in range(4)] for k in range(2)]
        blank = jnp.zeros((TILE, TILE), BF16)
        for i in range(2):
            r = i * 2 * TILE
            outs = []
            gained = [et[r + m * TILE : r + (m + 1) * TILE, r + m * TILE :] for m in range(2)]
            for k in range(2):
                grads = nt(left[k][r : r + 2 * TILE], right[k][r:])
                highs, lows = [], []
                for m in range(2):
                    q = r + m * TILE
                    grad = grads[m * TILE : (m + 1) * TILE, m * TILE :]
                    column = lx[q : q + TILE, tile_of(2 * p + k)]
                    row = lrow[2 * p + k][:, q:]
                    decay = []
                    for j in range((TOK - q) // TILE):
                        gap = row[:, j * TILE : (j + 1) * TILE] - column
                        decay.append(jnp.exp2(jnp.minimum(gap, 0.0) if j == 0 else gap))
                    decay = jnp.concatenate(decay, axis=1)
                    weight = decay * cbt[q : q + TILE, q:]
                    gained[m] = gained[m] + decay * grad
                    sums = jnp.sum(weight * grad, axis=0, keepdims=True)
                    for j in range((TOK - q) // TILE):
                        at = q // TILE + j
                        zs[k][at] = zs[k][at] + sums[:, j * TILE : (j + 1) * TILE]
                    wh, wl = split(weight)
                    highs.append(jnp.concatenate([blank, wh], axis=1) if m else wh)
                    lows.append(jnp.concatenate([blank, wl], axis=1) if m else wl)
                out = nn(jnp.concatenate(highs, axis=0), dycat[r:])
                low = nn(jnp.concatenate(lows, axis=0), dyh[r:])
                outs.append(out[:, :TILE] + out[:, TILE:] + low)
            for m in range(2):
                q = r + m * TILE
                et[q : q + TILE, q:] = gained[m]
            dx_ref[r : r + 2 * TILE, tile] = jnp.where(first, outs[0], outs[1])
        sh, sl = split(s0_ref[tile, :])
        both = nt(
            c_both,
            jnp.concatenate(
                [jnp.concatenate([sh, sh], axis=1), jnp.concatenate([sl, sl], axis=1)], axis=0
            ),
        )
        entering = both[:, :TILE] + both[:, TILE:]
        e = eh[:, tile].astype(F32) + el[:, tile].astype(F32)
        vh, vl = split(xv * dx_ref[:, tile] - e * entering)
        za, zb = jnp.concatenate(zs[0], axis=1), jnp.concatenate(zs[1], axis=1)
        v_ref[p] = (
            nt(picker, jnp.concatenate([vh, vl], axis=1))
            - jnp.where(sub == 0, za, jnp.where(sub == 1, zb, 0.0))
        )
        return carry

    for load in rest:
        load.wait()

    def line_scan(k):
        for copy in z_copies[k]:
            copy.wait()
        state = jnp.zeros((SLICE, PART), F32)
        for j in reversed(range(ZN)):
            inside[k, j] = state
            state = zbuf[k, j] + step[j][:, lanes_of(k)] * state
        xg[k, x] = state
        return [
            send(xg.at[k, x], xg.at[k, x], x_s.at[k, d], x_r.at[k, d], peer(q, z, core))
            for q, d in zip(x_peers, range(XN - 1))
        ]

    def line_back(k, copies):
        for copy in copies:
            copy.wait()
        entering = jnp.zeros((SLICE, PART), F32)
        for q in reversed(range(1, XN)):
            entering = jnp.where(q > x, xg[k, q] + xl[q][:, lanes_of(k)] * entering, entering)
        for j in range(ZN):
            lbuf[k, j] = inside[k, j] + fac[j][:, lanes_of(k)] * entering
        copies = [
            send(lbuf.at[k, q], back.at[k, z], b_s.at[k, d], b_r.at[k, d], peer(x, q, core))
            for q, d in zip(z_peers, range(ZN - 1))
        ]
        back[k, z] = lbuf[k, z]
        return copies

    lax.fori_loop(0, CUTS[0], inner, 0)
    x_copies = [line_scan(0)]
    lax.fori_loop(CUTS[0], CUTS[1], inner, 0)
    for copy in r_copies:
        copy.wait()
    b_copies = [line_back(0, x_copies[0])]
    lax.fori_loop(CUTS[1], CUTS[2], inner, 0)
    x_copies.append(line_scan(1))
    lax.fori_loop(CUTS[2], CUTS[3], inner, 0)
    b_copies.append(line_back(1, x_copies[1]))
    lax.fori_loop(CUTS[3], PAIRS, inner, 0)

    part = TOK // HN
    here = pl.ds(pl.multiple_of(hd * part, part), part)

    def scatter(own, got, k):
        return [
            send(own.at[q], got.at[d], y_s.at[k, d], y_r.at[k, d], (me, q))
            for q, d in zip(y_peers, range(HN - 1))
        ]

    def gather(own, got, out, k):
        out[here, :] = own[hd] + got[0] + got[1] + got[2]
        return [
            send(out.at[here], out.at[here], y_s.at[k, d], y_r.at[k, d], (me, q))
            for q, d in zip(y_peers, range(HN - 1))
        ]

    table = jnp.where(causal, et[...], 0.0)
    s_pair = split(s0_ref[...])
    dc = nn3(split(table.T), b_pair) + nn3((eh[...], el[...]), s_pair)
    for q in range(HN):
        own_c[q] = dc[q * part : (q + 1) * part]
    c_copies = scatter(own_c, got_c, 0)
    dbl[...] = nn3(split(table), c_pair)

    f_copies = []
    for k in range(PARTS):
        for copy in b_copies[k]:
            copy.wait()
        for j in range(ZN):
            late = back[k, j]
            early = g1[k, j] + a1[:, lanes_of(k)] * late
            rows = pl.ds(pl.multiple_of(core * HALF + j * SLICE, SLICE), SLICE)
            lat[k, rows, :] = jnp.where(even, early, late)
            other[k, j * SLICE : (j + 1) * SLICE, :] = jnp.where(even, late, early)
        f_copies.append(
            send(other.at[k], lat.at[k, mine], pair_s.at[1, k], pair_r.at[1, k], mate)
        )
    for copy in c_copies:
        copy.wait()
    c_copies = gather(own_c, got_c, dc_ref, 1)
    db = dbl[...]
    for k in range(PARTS):
        f_copies[k].wait()
        hi, lo = split(lat[k])
        lh[k] = hi
        ll[k] = lo
        both = nt(txh[:, lanes_of(k)], jnp.concatenate([hi, lo], axis=0))
        db = db + both[:, :STATE] + both[:, STATE:] + nt(txl[:, lanes_of(k)], hi)
    for q in range(HN):
        own_b[q] = db[q * part : (q + 1) * part]
    d_copies = scatter(own_b, got_b, 2)

    top = iota((8, TILE), 0)

    def corrector(k):
        def correct(p, carry):
            tile = tile_of(p + k * PART_PAIRS)
            spot = tile_of(p)
            late = jnp.concatenate([lh[k, :, spot], ll[k, :, spot]], axis=1)
            raw = nn(b_both, jnp.concatenate([late, late], axis=0))
            raw = raw[:, :TILE] + raw[:, TILE:]
            dx_ref[:, tile] = dx_ref[:, tile] + tail_ref[:, tile] * raw
            tx = txh[:, tile].astype(F32) + txl[:, tile].astype(F32)
            vh, vl = split(tx * raw)
            slot = pl.ds(pl.multiple_of((p + k * PART_PAIRS) * 8, 8), 8)
            w[slot, :] = v_ref[p + k * PART_PAIRS] + nt(
                picker, jnp.concatenate([vh, vl], axis=1)
            )
            eg = (a_ref[:, tile] * lat[k, :, spot] + gt_ref[k, :, spot]).T
            eg_ref[tile, :] = eg
            product = eg * s0_ref[tile, :]
            one = jnp.sum(jnp.sum(product[:WIDTH], axis=0, keepdims=True), axis=1, keepdims=True)
            two = jnp.sum(jnp.sum(product[WIDTH:], axis=0, keepdims=True), axis=1, keepdims=True)
            first_g[slot, :] = jnp.where(top == 0, one, jnp.where(top == 1, two, 0.0))
            return carry

        return correct

    lax.fori_loop(0, PART_PAIRS, corrector(0), 0)
    for copy in d_copies:
        copy.wait()
    d_copies = gather(own_b, got_b, db_ref, 3)
    lax.fori_loop(0, PART_PAIRS, corrector(1), 0)
    rates = prefix_sums(w[...], True) + first_g[:, 0:1]
    for h in range(HEADS):
        k = (h // 2) * 8 + h % 2
        dld_ref[h : h + 1, :] = rates[k : k + 1, :]
    for copy in c_copies:
        copy.wait()
    for copy in d_copies:
        copy.wait()


def run(x, ld, b, c, s0, dy):
    vm = pl.BlockSpec(memory_space=pltpu.VMEM)
    hbm = pl.BlockSpec(memory_space=pltpu.HBM)
    dma = pltpu.SemaphoreType.DMA
    shape = jax.ShapeDtypeStruct
    slab = pltpu.VMEM((PARTS, ZN, SLICE, PART), F32)
    half = pltpu.VMEM((PARTS, HALF, PART), F32)
    rows8 = pltpu.VMEM((ZN, 1, ROWS), F32)
    tall = pltpu.VMEM((TOK, ROWS), F32)
    tall16 = pltpu.VMEM((TOK, ROWS), BF16)
    state = pltpu.VMEM((PARTS, STATE, PART), F32)
    state16 = pltpu.VMEM((PARTS, STATE, PART), BF16)
    quarter = TOK // HN
    return pl.pallas_call(
        main_kernel,
        out_shape=(
            pltpu.VMEM((TOK, ROWS), F32),
            pltpu.VMEM((HEADS, TOK), F32),
            pltpu.VMEM((TOK, STATE), F32),
            pltpu.VMEM((TOK, STATE), F32),
            pltpu.VMEM((ROWS, STATE), F32),
        ),
        in_specs=[hbm] * 6,
        out_specs=(vm,) * 5,
        scratch_shapes=[
            tall,
            pltpu.VMEM((ROWS, STATE), F32),
            tall,
            state,
            pltpu.VMEM((1, ROWS), F32),
            tall16,
            tall16,
            tall,
            pltpu.VMEM((PAIRS, 8, TOK), F32),
            pltpu.VMEM((TOK, STATE), F32),
            pltpu.VMEM((HEADS, TOK), F32),
            pltpu.VMEM((TOK, STATE), F32),
            pltpu.VMEM((TOK, STATE), F32),
            pltpu.VMEM((32, TOK), F32),
            pltpu.VMEM((TILE, ROWS), BF16),
            pltpu.VMEM((TOK, HEADS * TILE), F32),
            pltpu.VMEM((HEADS, 1, TOK), F32),
            pltpu.VMEM((TOK, TOK), F32),
            pltpu.VMEM((TOK, TOK), F32),
            tall16,
            tall16,
            half,
            slab,
            slab,
            slab,
            pltpu.VMEM((LINE, 1, TILE), F32),
            pltpu.VMEM((LINE, 1, ROWS), F32),
            slab,
            rows8,
            rows8,
            pltpu.VMEM((PARTS, XN, SLICE, PART), F32),
            pltpu.VMEM((XN, 1, ROWS), F32),
            slab,
            slab,
            half,
            state,
            state16,
            state16,
            pltpu.VMEM((PAIRS * 8, TOK), F32),
            pltpu.VMEM((PAIRS * 8, TILE), F32),
            pltpu.VMEM((HN, quarter, STATE), F32),
            pltpu.VMEM((HN - 1, quarter, STATE), F32),
            pltpu.VMEM((HN, quarter, STATE), F32),
            pltpu.VMEM((HN - 1, quarter, STATE), F32),
            dma((PARTS + 5,)),
            dma((2, PARTS)), dma((2, PARTS)),
            dma((LINE - 1,)), dma((LINE - 1,)),
            dma((PARTS, ZN - 1)), dma((PARTS, ZN - 1)),
            dma((PARTS + 1, XN - 1)), dma((PARTS + 1, XN - 1)),
            dma((PARTS, ZN - 1)), dma((PARTS, ZN - 1)),
            dma((4, HN - 1)), dma((4, HN - 1)),
        ],
        compiler_params=pltpu.CompilerParams(
            collective_id=0, has_side_effects=True, vmem_limit_bytes=VMEM_LIMIT
        ),
        name="main",
    )(x, ld, b, c, s0, dy)


def out_kernel(*refs):
    sem = refs[-1]
    half = (len(refs) - 1) // 2
    copies = [
        pltpu.make_async_copy(refs[k], refs[half + k], sem.at[k]) for k in range(half)
    ]
    for copy in copies:
        copy.start()
    for copy in copies:
        copy.wait()


def store(*values):
    return pl.pallas_call(
        out_kernel,
        out_shape=tuple(jax.ShapeDtypeStruct(v.shape, v.dtype) for v in values),
        in_specs=[pl.BlockSpec(memory_space=pltpu.VMEM)] * len(values),
        out_specs=(pl.BlockSpec(memory_space=pltpu.HBM),) * len(values),
        scratch_shapes=[pltpu.SemaphoreType.DMA((len(values),))],
        compiler_params=pltpu.CompilerParams(vmem_limit_bytes=1024 * 1024),
        name="store",
    )(*values)


def per_device(inputs, log_decay, b_proj, c_proj, entry_states, out_grad):
    s0 = entry_states.reshape(ROWS, STATE)
    dx, dld, db, dc, eg = store(*run(inputs, log_decay, b_proj, c_proj, s0, out_grad))
    return (dx, dld, db, dc, eg.reshape(1, HEADS, WIDTH, STATE))


def solution(mesh):
    return jax.shard_map(
        per_device,
        mesh=mesh,
        in_specs=(
            P("seq", "head"),
            P("head", "seq"),
            P("seq", None),
            P("seq", None),
            P("seq", "head", None, None),
            P("seq", "head"),
        ),
        out_specs=(
            P("seq", "head"),
            P("head", "seq"),
            P("seq", None),
            P("seq", None),
            P("seq", "head", None, None),
        ),
        check_vma=False,
    )
```

time: 61.7 us -> 52.9 us (0.86); the launches traced: 61.6 us -> 51.9 us
  Pallas kernels: 56.6 us -> 51.3 us
  local copies, waits for them, and re-layouts: 4.35 us -> 0 us
    pallas_call x1 -> x2, Pallas kernels: 56.6 us -> 51.3 us  [the longest x1 49.4 us: run(): pl.pallas_call(main_kernel, out_shape=(pltpu.VMEM((TOK, ROWS), F32), pltp...]
    unnamed x5 -> x0, local copies, waits for them, and re-layouts: 4.35 us -> none
where the time goes in v2:
time: 52.9 us; the launch traced here: 51.9 us
  Pallas kernels  51.3 us (97%)
  between operations  0.64 us (1%)
    pallas_call x1, Pallas kernels, run(): pl.pallas_call(main_kernel, out_shape=(pltpu.VMEM((TOK, ROWS), F32), pltp...  49.4 us
    pallas_call x1, Pallas kernels, store(): pl.pallas_call(out_kernel, out_shape=tuple((jax.ShapeDtypeStruct(v.shape,...  1.93 us

profile of v2, /device:TPU:16, one launch (start us, length us, event | category | flops | bytes accessed | tf_op | source)
XLA Modules:
  0.0 51.9 jit_solution(14453982912853929754)
XLA Ops:
  0.6 49.4 %main.1 = (f32[512,1280]{1,0:T(8,128)S(1)}, f32[20,512]{1,0:T(8,128)S(1)}, f32[512,128]{1,0:T(8,128)S(1)}, f32[512,128]{1,0:T(8,128)S(1)}, f32[1280,128]{1,0:T(8,128)S(1)}) custom-call(f32[512,1280]{1,0:T(8,128)} %x_hbm.1, f32[20,512]{1,0:T(8,128)} %ld_hbm.1, f32[512,128]{1,0:T(8,128)} %b_hbm.1, f32[512,128]{1,0:T(8,128)} %c_hbm.1, f32[1280,128]{1,0:T(8,128)} %bitcast.2, ...), custom_call_target="tpu_custom_call" | custom-call | tf_op jit(solution)/shard_map/main/pallas_call | solution.py:492
  50.0 1.9 %store.1 = (f32[512,1280]{1,0:T(8,128)}, f32[20,512]{1,0:T(8,128)}, f32[512,128]{1,0:T(8,128)}, f32[512,128]{1,0:T(8,128)}, f32[1280,128]{1,0:T(8,128)}) custom-call(f32[512,1280]{1,0:T(8,128)S(1)} %get-tuple-element.15.refs_0_, f32[20,512]{1,0:T(8,128)S(1)} %get-tuple-element.16.refs_1_, f32[512,128]{1,0:T(8,128)S(1)} %get-tuple-element.17.refs_2_, ...), custom_call_target="tpu_custom_call" | custom-call | tf_op jit(solution)/shard_map/store/pallas_call | solution.py:576

commit v3 on v2

--- a/solution.py
+++ b/solution.py
@@ -27,7 +27,7 @@
 PARTS = 2
 PART_PAIRS = PAIRS // PARTS
 PART = PART_PAIRS * TILE
-CUTS = (4, 7, 7, 10)
+CUTS = (4, 7, 7, 9)
 VMEM_LIMIT = 58 * 1024 * 1024
 
 
@@ -113,9 +113,9 @@
     mate = peer(x, z, 1 - core)
     spot = z * 2 + core
     line = [lax.rem(spot + d, LINE) for d in range(1, LINE)]
-    z_peers = [lax.rem(z + d, ZN) for d in range(1, ZN)]
-    x_peers = [lax.rem(x + d, XN) for d in range(1, XN)]
-    y_peers = [lax.rem(hd + d, HN) for d in range(1, HN)]
+    z_peers = [lax.rem(z + d, ZN) for d in (4, 3, 5, 2, 6, 1, 7)]
+    x_peers = [lax.rem(x + d, XN) for d in (2, 1, 3)]
+    y_peers = [lax.rem(hd + d, HN) for d in (2, 1, 3)]
     barrier = pltpu.get_barrier_semaphore()
     everyone = (
         [peer(x, q // 2, lax.rem(q, 2)) for q in line]
@@ -142,6 +142,7 @@
     smalls[2].start()
     for device in everyone:
         pl.semaphore_signal(barrier, inc=1, device_id=device, device_id_type=MESH)
+
     def send(src, dst, s, r, device):
         copy = pltpu.make_async_remote_copy(
             src_ref=src, dst_ref=dst, send_sem=s, recv_sem=r, device_id=device, device_id_type=MESH
@@ -163,11 +164,6 @@
     columns = stack.T
     zl3[spot] = columns[TOK - 1 : TOK, :]
     columns = columns.astype(BF16)
-    pl.semaphore_wait(barrier, len(everyone))
-    l_copies = [
-        send(zl3.at[spot], zl3.at[spot], l_s.at[d], l_r.at[d], peer(x, q // 2, lax.rem(q, 2)))
-        for q, d in zip(line, range(LINE - 1))
-    ]
     narrow = (TILE, ROWS)
     spread = jnp.where((iota(narrow, 0) & 31) == (iota(narrow, 1) >> 6), 1.0, 0.0).astype(BF16)
     lanes[...] = spread
@@ -197,6 +193,12 @@
     for k in range(PARTS):
         loads[k].wait()
         lax.fori_loop(0, PART_PAIRS, starter(k), 0)
+        if k == 0:
+            pl.semaphore_wait(barrier, len(everyone))
+            l_copies = [
+                send(zl3.at[spot], zl3.at[spot], l_s.at[d], l_r.at[d], peer(x, q // 2, lax.rem(q, 2)))
+                for q, d in zip(line, range(LINE - 1))
+            ]
         m_copies.append(send(gt_ref.at[k, away], pg.at[k], pair_s.at[0, k], pair_r.at[0, k], mate))
     rest = [
         pltpu.make_async_copy(x_hbm, x_ref, in_s.at[PARTS]),

time: 52.9 us -> 50.9 us (0.962)
  Pallas kernels: 51.3 us -> 49.3 us
    pallas_call x1, Pallas kernels: 49.4 us -> 47.4 us  [run(): pl.pallas_call(main_kernel, out_shape=(pltpu.VMEM((TOK, ROWS), F32), pltp...]
where the time goes in v3:
time: 50.9 us; the launch traced here: 49.9 us
  Pallas kernels  49.3 us (97%)
  between operations  0.64 us (1%)
    pallas_call x1, Pallas kernels, run(): pl.pallas_call(main_kernel, out_shape=(pltpu.VMEM((TOK, ROWS), F32), pltp...  47.4 us
    pallas_call x1, Pallas kernels, store(): pl.pallas_call(out_kernel, out_shape=tuple((jax.ShapeDtypeStruct(v.shape,...  1.93 us

profile of v3, /device:TPU:16, one launch (start us, length us, event | category | flops | bytes accessed | tf_op | source)
XLA Modules:
  0.0 49.9 jit_solution(11250021566902050061)
XLA Ops:
  0.6 47.4 %main.1 = (f32[512,1280]{1,0:T(8,128)S(1)}, f32[20,512]{1,0:T(8,128)S(1)}, f32[512,128]{1,0:T(8,128)S(1)}, f32[512,128]{1,0:T(8,128)S(1)}, f32[1280,128]{1,0:T(8,128)S(1)}) custom-call(f32[512,1280]{1,0:T(8,128)} %x_hbm.1, f32[20,512]{1,0:T(8,128)} %ld_hbm.1, f32[512,128]{1,0:T(8,128)} %b_hbm.1, f32[512,128]{1,0:T(8,128)} %c_hbm.1, f32[1280,128]{1,0:T(8,128)} %bitcast.2, ...), custom_call_target="tpu_custom_call" | custom-call | tf_op jit(solution)/shard_map/main/pallas_call | solution.py:494
  48.0 1.9 %store.1 = (f32[512,1280]{1,0:T(8,128)}, f32[20,512]{1,0:T(8,128)}, f32[512,128]{1,0:T(8,128)}, f32[512,128]{1,0:T(8,128)}, f32[1280,128]{1,0:T(8,128)}) custom-call(f32[512,1280]{1,0:T(8,128)S(1)} %get-tuple-element.15.refs_0_, f32[20,512]{1,0:T(8,128)S(1)} %get-tuple-element.16.refs_1_, f32[512,128]{1,0:T(8,128)S(1)} %get-tuple-element.17.refs_2_, ...), custom_call_target="tpu_custom_call" | custom-call | tf_op jit(solution)/shard_map/store/pallas_call | solution.py:578

commit v4 on v3

--- a/solution.py
+++ b/solution.py
@@ -27,7 +27,7 @@
 PARTS = 2
 PART_PAIRS = PAIRS // PARTS
 PART = PART_PAIRS * TILE
-CUTS = (4, 7, 7, 9)
+CUTS = (4, 7, 7, 8)
 VMEM_LIMIT = 58 * 1024 * 1024
 
 

time: 50.9 us -> 51.8 us (1.018)
  Pallas kernels: 49.3 us -> 50.6 us
    pallas_call x1, Pallas kernels: 47.4 us -> 48.7 us  [run(): pl.pallas_call(main_kernel, out_shape=(pltpu.VMEM((TOK, ROWS), F32), pltp...]
where the time goes in v4:
time: 51.8 us; the launch traced here: 51.3 us
  Pallas kernels  50.6 us (98%)
  between operations  0.64 us (1%)
    pallas_call x1, Pallas kernels, run(): pl.pallas_call(main_kernel, out_shape=(pltpu.VMEM((TOK, ROWS), F32), pltp...  48.7 us
    pallas_call x1, Pallas kernels, store(): pl.pallas_call(out_kernel, out_shape=tuple((jax.ShapeDtypeStruct(v.shape,...  1.93 us

profile of v4, /device:TPU:16, one launch (start us, length us, event | category | flops | bytes accessed | tf_op | source)
XLA Modules:
  0.0 51.3 jit_solution(4144197151070110325)
XLA Ops:
  0.6 48.7 %main.1 = (f32[512,1280]{1,0:T(8,128)S(1)}, f32[20,512]{1,0:T(8,128)S(1)}, f32[512,128]{1,0:T(8,128)S(1)}, f32[512,128]{1,0:T(8,128)S(1)}, f32[1280,128]{1,0:T(8,128)S(1)}) custom-call(f32[512,1280]{1,0:T(8,128)} %x_hbm.1, f32[20,512]{1,0:T(8,128)} %ld_hbm.1, f32[512,128]{1,0:T(8,128)} %b_hbm.1, f32[512,128]{1,0:T(8,128)} %c_hbm.1, f32[1280,128]{1,0:T(8,128)} %bitcast.2, ...), custom_call_target="tpu_custom_call" | custom-call | tf_op jit(solution)/shard_map/main/pallas_call | solution.py:494
  49.3 1.9 %store.1 = (f32[512,1280]{1,0:T(8,128)}, f32[20,512]{1,0:T(8,128)}, f32[512,128]{1,0:T(8,128)}, f32[512,128]{1,0:T(8,128)}, f32[1280,128]{1,0:T(8,128)}) custom-call(f32[512,1280]{1,0:T(8,128)S(1)} %get-tuple-element.15.refs_0_, f32[20,512]{1,0:T(8,128)S(1)} %get-tuple-element.16.refs_1_, f32[512,128]{1,0:T(8,128)S(1)} %get-tuple-element.17.refs_2_, ...), custom_call_target="tpu_custom_call" | custom-call | tf_op jit(solution)/shard_map/store/pallas_call | solution.py:578
